TPU v7x, 128 devices: a whole 4x4x4 slice. The times are simulated.
128 devices in a mesh: head: 8 (over z, y_lo), pts: 16 (over y_hi, x, core).
Axes of the slice: x: 4, y: 4 (y_hi: 2, y_lo: 2; y = y_hi * 2 + y_lo), z: 4, core: 2. Of those that a mesh axis runs over, the one named last changes fastest.
Arguments:
- layer_inputs_trainorder: bfloat16 [786432, 256], P(('head', 'pts')), may hold values from -6 to 6
- inference_placement: int32 [786432], P(('head', 'pts')), may hold values from 0 to 786431, as said below
- initial_layernorm_gain: float32 [256], replicated, may hold values from 0.1 to 1.9
- initial_layernorm_offset: float32 [256], replicated, may hold values from -2 to 2
- attribute_projection: bfloat16 [256, 256], replicated, may hold values from -0.375 to 0.375
- assignment_feeder_projection: bfloat16 [256, 256], replicated, may hold values from -0.375 to 0.375
- partition_projection: bfloat16 [16, 32], replicated, may hold values from -1.5 to 1.5
- partition_offset: float32 [32], replicated, may hold values from -4 to 4
- softmax_sharpness: float32 [16], P('head'), may hold values from 0.03 to 1
- partition_question_map: float32 [16, 16], replicated, may hold values from -1.5 to 1.5
- partition_lookup_map: float32 [16, 16], replicated, may hold values from -1.5 to 1.5
- partition_content_map: float32 [16, 16], replicated, may hold values from -1.5 to 1.5
- emitted_projection: bfloat16 [256, 256], replicated, may hold values from -0.375 to 0.375
- emitted_offset: float32 [256], replicated, may hold values from -2 to 2
- latter_layernorm_gain: float32 [256], replicated, may hold values from 0.1 to 1.9
- latter_layernorm_offset: float32 [256], replicated, may hold values from -2 to 2
- perceptron_entry_map: bfloat16 [256, 1024], replicated, may hold values from -0.375 to 0.375
- perceptron_entry_offset: float32 [1024], replicated, may hold values from -2 to 2
- perceptron_exit_map: bfloat16 [1024, 256], replicated, may hold values from -0.1875 to 0.1875
- perceptron_exit_offset: float32 [256], replicated, may hold values from -2 to 2
Outputs:
- served: bfloat16 [16, 49152, 256], P('pts', 'head')
Inputs may be any that keep to these rules, and one draw needn't show every extreme that they name: inference_placement is a permutation of all points; of the 6144 points of each aligned block of the training order, exactly 48 go to each aligned block of 6144 serving positions.
All inputs are finite; a program needn't handle non-finite values.
Results may differ from a plain program's by a relative error of at most 0.0035.
The roundings to bfloat16 on the way count: a program that leaves them out, or rounds other values in their place, can miss the bound.
Values may be sent and summed in bfloat16 or wider, within the bound.
A program may use at most 128 MiB of HBM per device.

v0:
```python
import math
import jax
import jax.numpy as jnp
from jax import lax
from jax.sharding import Mesh
from jax.sharding import PartitionSpec as P

DH = 16
HEAD_PTS = ("head_0", "head_1", "pts_0", "pts_1", "pts_2")
HEAD = ("head_0", "head_1")
PTS = ("pts_0", "pts_1", "pts_2")


def from_everyone(array, axis):
    copies = jnp.broadcast_to(array, (lax.axis_size(axis), *array.shape))
    return lax.all_to_all(copies, axis, split_axis=0, concat_axis=0, tiled=True)


def in_order(tiles, dim):
    tiles = jnp.moveaxis(tiles, 0, dim)
    dims = tiles.shape
    return tiles.reshape(*dims[:dim], dims[dim] * dims[dim + 1], *dims[dim + 2 :])


def gather_directly(array, axis, dim):
    tiles = from_everyone(array, axis)
    return in_order(tiles, dim)


def one_axis_at_a_time(array, axes):
    for axis in axes:
        array = lax.psum(array, axis)
    return array


def layer_norm(row_block, gain_vec, bias_vec):
    row_mean = jnp.mean(row_block, axis=-1, keepdims=True)
    centred = row_block - row_mean
    spread = jnp.mean(centred * centred, axis=-1, keepdims=True)
    return centred * lax.rsqrt(spread + 1e-05) * gain_vec + bias_vec


def move_rows(rows, labels, ordering):
    arrived = lax.all_to_all(rows[ordering], HEAD_PTS, split_axis=0, concat_axis=0, tiled=True)
    arrived_labels = lax.all_to_all(labels, HEAD_PTS, split_axis=0, concat_axis=0, tiled=True)
    placed = jnp.argsort(arrived_labels[:, 0])
    return (arrived[placed], arrived_labels[placed, 1])


def slice_attention(
    totals, numerator, partition_question_map, partition_lookup_map, partition_content_map
):
    slice_token = numerator / (totals + 1e-05)[:, :, None]
    highest_mode = lax.Precision.HIGHEST
    query_rows = jnp.einsum(
        "izn,nu->izu", slice_token, partition_question_map, precision=highest_mode
    )
    key_vectors = jnp.einsum(
        "izn,nu->izu", slice_token, partition_lookup_map, precision=highest_mode
    )
    value_rows = jnp.einsum(
        "izn,nu->izu", slice_token, partition_content_map, precision=highest_mode
    )
    score_scale = 1.0 / math.sqrt(DH)
    scores = (
        jnp.einsum("hme,hne->hmn", query_rows, key_vectors, precision=highest_mode) * score_scale
    )
    attention = jax.nn.softmax(scores, axis=-1)
    return jnp.einsum("hmn,hne->hme", attention, value_rows, precision=highest_mode).astype(
        jnp.bfloat16
    )


def finish_rows(
    residual_rows,
    blended_rows,
    emitted_projection,
    emitted_offset,
    latter_layernorm_gain,
    latter_layernorm_offset,
    perceptron_entry_map,
    perceptron_entry_offset,
    perceptron_exit_map,
    perceptron_exit_offset,
):
    hidden = (
        residual_rows.astype(jnp.float32)
        + jnp.dot(blended_rows, emitted_projection, preferred_element_type=jnp.float32)
        + emitted_offset
    )
    normed_two = layer_norm(hidden, latter_layernorm_gain, latter_layernorm_offset).astype(
        jnp.bfloat16
    )
    inner_act = jax.nn.gelu(
        jnp.dot(normed_two, perceptron_entry_map, preferred_element_type=jnp.float32)
        + perceptron_entry_offset,
        approximate=False,
    ).astype(jnp.bfloat16)
    return (
        hidden
        + jnp.dot(inner_act, perceptron_exit_map, preferred_element_type=jnp.float32)
        + perceptron_exit_offset
    ).astype(jnp.bfloat16)


def body(
    layer_inputs_trainorder,
    inference_placement,
    initial_layernorm_gain,
    initial_layernorm_offset,
    attribute_projection,
    assignment_feeder_projection,
    partition_projection,
    partition_offset,
    softmax_sharpness,
    partition_question_map,
    partition_lookup_map,
    partition_content_map,
    emitted_projection,
    emitted_offset,
    latter_layernorm_gain,
    latter_layernorm_offset,
    perceptron_entry_map,
    perceptron_entry_offset,
    perceptron_exit_map,
    perceptron_exit_offset,
):
    groups = lax.axis_size(HEAD)
    shards = lax.axis_size(PTS)
    local_rows = layer_inputs_trainorder.shape[0]
    model_width = layer_inputs_trainorder.shape[1]
    dest_block = inference_placement // local_rows
    target = dest_block % groups * shards + dest_block // groups
    ordering = jnp.argsort(target, stable=True)
    anchor = lax.axis_index(HEAD_PTS) * local_rows + jnp.arange(local_rows, dtype=jnp.int32)
    labels = jnp.stack([inference_placement[ordering], anchor[ordering]], axis=1)
    sharpness_sequence = gather_directly(softmax_sharpness, HEAD, 0)
    every_attender = sharpness_sequence.shape[0]
    standardized_entries = layer_norm(
        layer_inputs_trainorder.astype(jnp.float32),
        initial_layernorm_gain,
        initial_layernorm_offset,
    ).astype(jnp.bfloat16)
    slice_feature_rows = (
        jnp.dot(standardized_entries, attribute_projection, preferred_element_type=jnp.float32)
        .astype(jnp.bfloat16)
        .reshape(local_rows, every_attender, DH)
    )
    middle = (
        jnp.dot(
            standardized_entries, assignment_feeder_projection, preferred_element_type=jnp.float32
        )
        .astype(jnp.bfloat16)
        .reshape(local_rows, every_attender, DH)
    )
    partition_scores_raw = jnp.einsum(
        "rhd,dm->rhm", middle, partition_projection, preferred_element_type=jnp.float32
    )
    partition_scores_raw = (partition_scores_raw + partition_offset) / sharpness_sequence[:, None]
    coefficient_array = jax.nn.softmax(partition_scores_raw, axis=-1)
    coefficients_halfprecision = coefficient_array.astype(jnp.bfloat16)
    totals = jnp.sum(coefficient_array, axis=0)
    numerator = jnp.einsum(
        "qct,qcv->ctv",
        coefficients_halfprecision,
        slice_feature_rows,
        preferred_element_type=jnp.float32,
    )
    totals, numerator = (
        one_axis_at_a_time(totals, HEAD_PTS),
        one_axis_at_a_time(numerator, HEAD_PTS),
    )
    slice_output = slice_attention(
        totals, numerator, partition_question_map, partition_lookup_map, partition_content_map
    )
    blended_rows = (
        jnp.einsum(
            "fny,nyp->fnp",
            coefficients_halfprecision,
            slice_output,
            preferred_element_type=jnp.float32,
        )
        .astype(jnp.bfloat16)
        .reshape(local_rows, model_width)
    )
    result = finish_rows(
        layer_inputs_trainorder,
        blended_rows,
        emitted_projection,
        emitted_offset,
        latter_layernorm_gain,
        latter_layernorm_offset,
        perceptron_entry_map,
        perceptron_entry_offset,
        perceptron_exit_map,
        perceptron_exit_offset,
    )
    served, unused = move_rows(result, labels, ordering)
    return served[None]


def solution(mesh):
    torus = Mesh(
        mesh.devices.reshape(4, 2, 2, 4, 2), ("head_0", "head_1", "pts_0", "pts_1", "pts_2")
    )
    in_specs = (
        P(HEAD_PTS, None),
        P(HEAD_PTS),
        P(),
        P(),
        P(),
        P(),
        P(),
        P(),
        P(HEAD),
        P(),
        P(),
        P(),
        P(),
        P(),
        P(),
        P(),
        P(),
        P(),
        P(),
        P(),
    )
    out_specs = P(PTS, HEAD, None)
    return jax.shard_map(body, mesh=torus, in_specs=in_specs, out_specs=out_specs, check_vma=False)
```

profile of v0, /device:TPU:1, one launch (start us, length us, event | category | flops | bytes accessed | tf_op | source)
XLA Modules:
  0.0 388.4 jit_solution(6724094378203701550)
XLA Ops:
  0.0 1.3 broadcast_in_dim.8
  1.3 6.9 %all-to-all-start = ((f32[8,1,2]{2,1,0:T(1,128)}), f32[8,1,2]{2,1,0:T(1,128)S(1)}, u32[]{:S(2)}, u32[]{:S(2)}) async-start(f32[8,1,2]{2,1,0:T(1,128)} %broadcast_in_dim.8), calls=%async_computation | async-start | bytes 8192 | tf_op jit(solution)/shard_map/all_to_all | solution.py:16
  8.2 4.6 %copy.45 = bf16[6144,256]{0,1:T(8,128)(2,1)} copy(bf16[6144,256]{1,0:T(8,128)(2,1)} %param.20) | data formatting | bytes 6291456 | tf_op args[0]
  12.8 2.6 convert_reduce_fusion
  15.4 2.7 fusion.27
  18.2 5.3 %convolution_convert_fusion.2 = bf16[6144,256]{0,1:T(8,128)(2,1)} fusion(bf16[256,256]{1,0:T(8,128)(2,1)S(1)} %copy-done.12, bf16[6144,256]{0,1:T(8,128)(2,1)} %copy.45, f32[256]{0:T(256)S(1)} %copy-done.19, f32[256]{0:T(256)S(1)} %copy-done.20, f32[6144]{0:T(1024)S(1)} %add_rsqrt_fusion.1, f32[6144]{0:T(1024)S(1)} %broadcast_multiply_fusion.1), kind=kOutput, calls=%fused_computation.36 | convolution fusion | flops 816316416 | bytes 6473728 | tf_op jit(solution)/shard_map/dot_general | solution.py:150
  23.5 3.4 convolution_convert_fusion.1
  27.0 6.7 %sort.34 = (s32[6144]{0:T(1024)}, s32[6144]{0:T(1024)S(1)}) sort(s32[6144]{0:T(1024)S(1)} %fusion.46, s32[6144]{0:T(1024)S(1)} %iota.11), dimensions={0}, to_apply=%region_19.20 | sort | flops 79872 | bytes 98304 | tf_op jit(solution)/shard_map/jit(argsort)/sort | solution.py:134
  33.7 34.3 %gather_fusion.1 = s32[6144]{0:T(1024)S(1)} fusion(s32[6144]{0:T(1024)S(1)} %copy-done.2, s32[6144]{0:T(1024)S(1)} %get-tuple-element.27), kind=kCustom, calls=%fused_computation.1 | custom fusion | bytes 73728 | tf_op jit(solution)/shard_map/gather | solution.py:136
  68.1 34.3 %gather_fusion.2 = s32[6144]{0:T(1024)S(1)} fusion(s32[6144]{0:T(1024)S(1)} %get-tuple-element.28, s32[6144]{0:T(1024)S(1)} %get-tuple-element.27), kind=kCustom, calls=%fused_computation.2 | custom fusion | bytes 73728 | tf_op jit(solution)/shard_map/gather | solution.py:136
  102.6 0.8 copy.52
  103.3 11.3 %all-to-all-start.2 = ((s32[128,48,2]{1,2,0:T(2,128)}), s32[128,48,2]{1,2,0:T(2,128)}, u32[]{:S(2)}, u32[]{:S(2)}) async-start(s32[128,48,2]{1,2,0:T(2,128)} %copy.52), calls=%async_computation.2 | async-start | bytes 262144 | tf_op jit(solution)/shard_map/all_to_all | solution.py:45
  115.9 10.9 %fusion.93 = (f32[6144,16]{0,1:T(8,128)S(1)}, f32[6144,16,32]{0,2,1:T(8,128)}) fusion(bf16[6144,16,16]{0,2,1:T(8,128)(2,1)} %bitcast.48, f32[16]{0:T(128)S(1)} %div.64, f32[32]{0:T(128)S(1)} %copy-done.24, bf16[16,32]{1,0:T(8,128)(2,1)S(1)} %copy-done.17), kind=kOutput, calls=%fused_computation.125 | convolution fusion | flops 113246240 | bytes 16123072 | tf_op jit(solution)/shard_map/sub | solution.py:160
  126.8 9.1 %fusion.31 = (f32[16,32]{1,0:T(8,128)S(1)}, bf16[6144,16,32]{0,2,1:T(8,128)(2,1)}) fusion(f32[6144,16,32]{0,2,1:T(8,128)} %get-tuple-element.22, f32[6144,16]{0,1:T(8,128)S(1)} %get-tuple-element.21), kind=kLoop, calls=%fused_computation.47 | loop fusion | flops 9436672 | bytes 19269632 | tf_op jit(solution)/shard_map/reduce_sum | solution.py:162
  135.8 4.6 %fusion.98 = f32[16,32,16]{1,2,0:T(8,128)S(1)} fusion(bf16[6144,16,32]{0,2,1:T(8,128)(2,1)} %get-tuple-element.20, bf16[6144,16,16]{0,2,1:T(8,128)(2,1)S(1)} %bitcast.46), kind=kOutput, calls=%fused_computation.128 | convolution fusion | flops 100663296 | bytes 9469952 | tf_op jit(solution)/shard_map/qct,qcv->ctv/dot_general | solution.py:163
  140.4 15.4 %all-reduce.1 = (f32[16,32,16]{1,2,0:T(8,128)S(1)}, f32[16,32]{1,0:T(8,128)S(1)}) all-reduce(f32[16,32,16]{1,2,0:T(8,128)S(1)} %fusion.98, f32[16,32]{1,0:T(8,128)S(1)} %get-tuple-element.19), channel_id=1, replica_groups=mesh['head_0'=4,'head_1'=2,'pts_0'=2,'pts_1'=4,'pts_2'=2] {'head_0'}, use_global_device_ids=true, to_apply=%region_4.5 | all-reduce | flops 8704 | bytes 69632 | tf_op jit(solution)/shard_map/psum | solution.py:32
  155.8 7.7 %all-reduce.4 = (f32[16,32,16]{1,2,0:T(8,128)S(1)}, f32[16,32]{1,0:T(8,128)S(1)}) all-reduce(f32[16,32,16]{1,2,0:T(8,128)S(1)} %get-tuple-element.11, f32[16,32]{1,0:T(8,128)S(1)} %get-tuple-element.12), channel_id=1, replica_groups=mesh['head_0'=4,'head_1'=2,'pts_0'=2,'pts_1'=4,'pts_2'=2] {'head_1'}, use_global_device_ids=true, to_apply=%region_5.6 | all-reduce | flops 8704 | bytes 69632 | tf_op jit(solution)/shard_map/psum | solution.py:32
  163.5 10.4 %all-reduce.3 = (f32[16,32,16]{1,2,0:T(8,128)S(1)}, f32[16,32]{1,0:T(8,128)S(1)}) all-reduce(f32[16,32,16]{1,2,0:T(8,128)S(1)} %get-tuple-element.17, f32[16,32]{1,0:T(8,128)S(1)} %get-tuple-element.18), channel_id=1, replica_groups=mesh['head_0'=4,'head_1'=2,'pts_0'=2,'pts_1'=4,'pts_2'=2] {'pts_0'}, use_global_device_ids=true, to_apply=%region_6.7 | all-reduce | flops 8704 | bytes 69632 | tf_op jit(solution)/shard_map/psum | solution.py:32
  174.0 15.1 %all-reduce = (f32[16,32,16]{1,2,0:T(8,128)S(1)}, f32[16,32]{1,0:T(8,128)S(1)}) all-reduce(f32[16,32,16]{1,2,0:T(8,128)S(1)} %get-tuple-element.15, f32[16,32]{1,0:T(8,128)S(1)} %get-tuple-element.16), channel_id=1, replica_groups=mesh['head_0'=4,'head_1'=2,'pts_0'=2,'pts_1'=4,'pts_2'=2] {'pts_1'}, use_global_device_ids=true, to_apply=%region_7.8 | all-reduce | flops 8704 | bytes 69632 | tf_op jit(solution)/shard_map/psum | solution.py:32
  189.1 15.1 %all-reduce.2 = (f32[16,32,16]{1,2,0:T(8,128)S(1)}, f32[16,32]{1,0:T(8,128)S(1)}) all-reduce(f32[16,32,16]{1,2,0:T(8,128)S(1)} %get-tuple-element.9, f32[16,32]{1,0:T(8,128)S(1)} %get-tuple-element.10), channel_id=1, replica_groups=mesh['head_0'=4,'head_1'=2,'pts_0'=2,'pts_1'=4,'pts_2'=2] {'pts_2'}, use_global_device_ids=true, to_apply=%region_8.9 | all-reduce | flops 8704 | bytes 69632 | tf_op jit(solution)/shard_map/psum | solution.py:32
  206.2 3.7 convolution_convert_fusion
  210.1 1.4 fusion.95
  212.2 1.9 copy-done.5
  214.1 58.5 %fusion.119 = bf16[6144,1024]{1,0:T(8,128)(2,1)} fusion(f32[1024]{0:T(1024)S(1)} %copy-done.18, bf16[256,1024]{1,0:T(8,128)(2,1)S(1)} %copy-done, f32[6144,256]{0,1:T(8,128)S(1)} %get-tuple-element.26, f32[256]{0:T(256)S(1)} %copy-done.21, f32[256]{0:T(256)S(1)} %copy-done.22, f32[6144]{0:T(1024)S(1)} %add_rsqrt_fusion, ...), kind=kOutput, calls=%fused_computation.8.clone.clone.clone.clone.clone.clone.clone.clone.1 | convolution fusion | flops 3644325888 | bytes 19453952 | tf_op jit(solution)/shard_map/dot_general | solution.py:95
  272.6 15.5 %fusion.22 = bf16[6144,256]{0,1:T(8,128)(2,1)} fusion(f32[6144,256]{0,1:T(8,128)} %copy-done.5, bf16[1024,256]{1,0:T(8,128)(2,1)S(1)} %copy-done.11, f32[256]{0:T(256)S(1)} %copy-done.23, bf16[6144,1024]{1,0:T(8,128)(2,1)} %fusion.119), kind=kOutput, calls=%fused_computation.37 | convolution fusion | flops 3225944064 | bytes 22545408 | tf_op jit(solution)/shard_map/dot_general | solution.py:101
  288.1 3.2 copy.51
  291.3 25.1 %gather_fusion = bf16[6144,256]{1,0:T(8,128)(2,1)} fusion(bf16[6144,256]{1,0:T(8,128)(2,1)S(1)} %copy.51, s32[6144]{0:T(1024)S(1)} %copy-done.8), kind=kCustom, calls=%fused_computation | custom fusion | bytes 6316032 | tf_op jit(solution)/shard_map/gather | solution.py:44
  316.4 4.7 %all-to-all-start.1 = ((bf16[128,48,256]{2,1,0:T(8,128)(2,1)}), bf16[128,48,256]{2,1,0:T(8,128)(2,1)}, u32[]{:S(2)}, u32[]{:S(2)}) async-start(bf16[128,48,256]{2,1,0:T(8,128)(2,1)} %bitcast.45), calls=%async_computation.1 | async-start | bytes 6291456 | tf_op jit(solution)/shard_map/all_to_all | solution.py:44
  321.1 0.9 copy.53
  322.2 6.7 %sort.35 = (s32[6144]{0:T(1024)}, s32[6144]{0:T(1024)S(1)}) sort(s32[6144]{0:T(1024)S(1)} %bitcast.47, s32[6144]{0:T(1024)S(1)} %iota.13), dimensions={0}, to_apply=%region_20.21 | sort | flops 79872 | bytes 98304 | tf_op jit(solution)/shard_map/jit(argsort)/sort | solution.py:46
  328.9 33.4 %all-to-all-done.1 = bf16[128,48,256]{2,1,0:T(8,128)(2,1)} async-done(((bf16[128,48,256]{2,1,0:T(8,128)(2,1)}), bf16[128,48,256]{2,1,0:T(8,128)(2,1)}, u32[]{:S(2)}, u32[]{:S(2)}) %all-to-all-start.1) | async-done | bytes 3145760 | tf_op jit(solution)/shard_map/all_to_all | solution.py:44
  362.3 25.9 %gather_fusion.3 = bf16[6144,256]{1,0:T(8,128)(2,1)} fusion(bf16[6144,256]{1,0:T(8,128)(2,1)} %bitcast.9, s32[6144]{0:T(1024)S(1)} %fusion.48), kind=kCustom, calls=%fused_computation.3 | custom fusion | bytes 6316032 | tf_op jit(solution)/shard_map/gather | solution.py:47
  (76 shorter events, 4.5 us)
Async XLA Ops:
  0.0 214.1 %copy-start = (bf16[256,1024]{1,0:T(8,128)(2,1)S(1)}, bf16[256,1024]{1,0:T(8,128)(2,1)}, u32[]{:S(2)}) copy-start(bf16[256,1024]{1,0:T(8,128)(2,1)} %param.36) | copy-start | bytes 1572868
  0.0 18.2 %copy-start.20 = (f32[256]{0:T(256)S(1)}, f32[256]{0:T(256)}, u32[]{:S(2)}) copy-start(f32[256]{0:T(256)} %param.22) | copy-start | bytes 3076
  0.0 18.2 %copy-start.19 = (f32[256]{0:T(256)S(1)}, f32[256]{0:T(256)}, u32[]{:S(2)}) copy-start(f32[256]{0:T(256)} %param.23) | copy-start | bytes 3076
  0.0 18.2 %copy-start.12 = (bf16[256,256]{1,0:T(8,128)(2,1)S(1)}, bf16[256,256]{1,0:T(8,128)(2,1)}, u32[]{:S(2)}) copy-start(bf16[256,256]{1,0:T(8,128)(2,1)} %param.25) | copy-start | bytes 393220
  1.3 102.0 %all-to-all-start = ((f32[8,1,2]{2,1,0:T(1,128)}), f32[8,1,2]{2,1,0:T(1,128)S(1)}, u32[]{:S(2)}, u32[]{:S(2)}) async-start(f32[8,1,2]{2,1,0:T(1,128)} %broadcast_in_dim.8), calls=%async_computation | async-start | bytes 8192 | tf_op jit(solution)/shard_map/all_to_all | solution.py:16
  12.8 10.7 %copy-start.3 = (bf16[6144,256]{0,1:T(8,128)(2,1)S(1)}, bf16[6144,256]{0,1:T(8,128)(2,1)}, u32[]{:S(2)}) copy-start(bf16[6144,256]{0,1:T(8,128)(2,1)} %copy.45) | copy-start | bytes 9437188
  12.8 10.7 %copy-start.13 = (bf16[256,256]{1,0:T(8,128)(2,1)S(1)}, bf16[256,256]{1,0:T(8,128)(2,1)}, u32[]{:S(2)}) copy-start(bf16[256,256]{1,0:T(8,128)(2,1)} %param.24) | copy-start | bytes 393220
  18.2 8.7 %copy-start.2 = (s32[6144]{0:T(1024)S(1)}, s32[6144]{0:T(1024)}, u32[]{:S(2)}) copy-start(s32[6144]{0:T(1024)} %param.21) | copy-start | bytes 73732
  33.7 34.3 %copy-start.7 = (s32[6144]{0:T(1024)}, s32[6144]{0:T(1024)S(1)}, u32[]{:S(2)}) copy-start(s32[6144]{0:T(1024)S(1)} %get-tuple-element.27) | copy-start | bytes 73732
  68.1 47.8 %copy-start.17 = (bf16[16,32]{1,0:T(8,128)(2,1)S(1)}, bf16[16,32]{1,0:T(8,128)(2,1)}, u32[]{:S(2)}) copy-start(bf16[16,32]{1,0:T(8,128)(2,1)} %param.26) | copy-start | bytes 3076
  68.1 47.8 %copy-start.24 = (f32[32]{0:T(128)S(1)}, f32[32]{0:T(128)}, u32[]{:S(2)}) copy-start(f32[32]{0:T(128)} %param.27) | copy-start | bytes 388
  103.3 213.1 %all-to-all-start.2 = ((s32[128,48,2]{1,2,0:T(2,128)}), s32[128,48,2]{1,2,0:T(2,128)}, u32[]{:S(2)}, u32[]{:S(2)}) async-start(s32[128,48,2]{1,2,0:T(2,128)} %copy.52), calls=%async_computation.2 | async-start | bytes 262144 | tf_op jit(solution)/shard_map/all_to_all | solution.py:45
  126.8 9.1 %copy-start.6 = (bf16[6144,256]{0,1:T(8,128)(2,1)S(1)}, bf16[6144,256]{0,1:T(8,128)(2,1)}, u32[]{:S(2)}) copy-start(bf16[6144,256]{0,1:T(8,128)(2,1)} %convolution_convert_fusion.1) | copy-start | bytes 9437188
  126.8 77.4 %copy-start.14 = (f32[16,16]{1,0:T(8,128)S(1)}, f32[16,16]{1,0:T(8,128)}, u32[]{:S(2)}) copy-start(f32[16,16]{1,0:T(8,128)} %param.30) | copy-start | bytes 3076
  126.8 77.7 %copy-start.15 = (f32[16,16]{1,0:T(8,128)S(1)}, f32[16,16]{1,0:T(8,128)}, u32[]{:S(2)}) copy-start(f32[16,16]{1,0:T(8,128)} %param.29) | copy-start | bytes 3076
  126.8 78.0 %copy-start.16 = (f32[16,16]{1,0:T(8,128)S(1)}, f32[16,16]{1,0:T(8,128)}, u32[]{:S(2)}) copy-start(f32[16,16]{1,0:T(8,128)} %param.31) | copy-start | bytes 3076
  135.8 74.2 %copy-start.9 = (bf16[256,256]{1,0:T(8,128)(2,1)S(1)}, bf16[256,256]{1,0:T(8,128)(2,1)}, u32[]{:S(2)}) copy-start(bf16[256,256]{1,0:T(8,128)(2,1)} %param.32) | copy-start | bytes 393220
  135.8 74.2 %copy-start.10 = (f32[256]{0:T(256)S(1)}, f32[256]{0:T(256)}, u32[]{:S(2)}) copy-start(f32[256]{0:T(256)} %param.33) | copy-start | bytes 3076
  204.1 5.9 %copy-start.4 = (bf16[6144,256]{0,1:T(8,128)(2,1)S(1)}, bf16[6144,256]{0,1:T(8,128)(2,1)}, u32[]{:S(2)}) copy-start(bf16[6144,256]{0,1:T(8,128)(2,1)} %copy.45) | copy-start | bytes 9437188
  210.0 4.1 %copy-start.18 = (f32[1024]{0:T(1024)S(1)}, f32[1024]{0:T(1024)}, u32[]{:S(2)}) copy-start(f32[1024]{0:T(1024)} %param.37) | copy-start | bytes 12292
  210.0 4.1 %copy-start.21 = (f32[256]{0:T(256)S(1)}, f32[256]{0:T(256)}, u32[]{:S(2)}) copy-start(f32[256]{0:T(256)} %param.35) | copy-start | bytes 3076
  210.0 4.1 %copy-start.22 = (f32[256]{0:T(256)S(1)}, f32[256]{0:T(256)}, u32[]{:S(2)}) copy-start(f32[256]{0:T(256)} %param.34) | copy-start | bytes 3076
  211.5 2.6 copy-start.5
  214.1 58.5 %copy-start.11 = (bf16[1024,256]{1,0:T(8,128)(2,1)S(1)}, bf16[1024,256]{1,0:T(8,128)(2,1)}, u32[]{:S(2)}) copy-start(bf16[1024,256]{1,0:T(8,128)(2,1)} %param.38) | copy-start | bytes 1572868
  214.1 58.5 %copy-start.23 = (f32[256]{0:T(256)S(1)}, f32[256]{0:T(256)}, u32[]{:S(2)}) copy-start(f32[256]{0:T(256)} %param.39) | copy-start | bytes 3076
  272.6 18.7 %copy-start.8 = (s32[6144]{0:T(1024)S(1)}, s32[6144]{0:T(1024)}, u32[]{:S(2)}) copy-start(s32[6144]{0:T(1024)} %copy-done.7) | copy-start | bytes 73732
  316.4 45.9 %all-to-all-start.1 = ((bf16[128,48,256]{2,1,0:T(8,128)(2,1)}), bf16[128,48,256]{2,1,0:T(8,128)(2,1)}, u32[]{:S(2)}, u32[]{:S(2)}) async-start(bf16[128,48,256]{2,1,0:T(8,128)(2,1)} %bitcast.45), calls=%async_computation.1 | async-start | bytes 6291456 | tf_op jit(solution)/shard_map/all_to_all | solution.py:44
  362.3 25.9 %copy-start.1 = (bf16[256,1024]{1,0:T(8,128)(2,1)S(1)}, bf16[256,1024]{1,0:T(8,128)(2,1)}, u32[]{:S(2)}) copy-start(bf16[256,1024]{1,0:T(8,128)(2,1)} %param.36) | copy-start | bytes 1572868
where the time goes:
time: 396 us; the launch traced here: 388 us
  local copies, waits for them, and re-layouts  133 us (34%)
  matrix products  105 us (27%)
  blocking collectives  63.7 us (16%)
  waiting for transfers between devices  33.4 us (8%)
  other arithmetic  29.4 us (7%)
  starting transfers between devices  22.8 us (6%)
    psum x5, blocking collectives, one_axis_at_a_time(): array = lax.psum(array, axis)  63.7 us
    dot_general x1, matrix products, finish_rows(): jnp.dot(normed_two, perceptron_entry_map, preferred_element_type=jnp.floa...  58.5 us
    gather x1, local copies, waits for them, and re-layouts, body(): inference_placement[ordering]  34.3 us
    gather x1, local copies, waits for them, and re-layouts, body(): anchor[ordering]  34.3 us
    all_to_all x1, waiting for transfers between devices, move_rows(): lax.all_to_all(rows[ordering], HEAD_PTS, split_axis=0, concat_axis=0, til...  33.4 us
    gather x1, local copies, waits for them, and re-layouts, move_rows(): return (arrived[placed], arrived_labels[placed, 1])  25.9 us
    gather x1, local copies, waits for them, and re-layouts, move_rows(): rows[ordering]  25.1 us
    dot_general x1, matrix products, finish_rows(): jnp.dot(inner_act, perceptron_exit_map, preferred_element_type=jnp.float32)  15.5 us
  transfers between devices with their start and end apart: 3, of which 1 were waited for; matrix products, arithmetic and copies ran while one was open for 61% of the time, Pallas kernels for 0%

commit v1 on v0

--- a/solution.py
+++ b/solution.py
@@ -29,7 +29,7 @@
 
 def one_axis_at_a_time(array, axes):
     for axis in axes:
-        array = lax.psum(array, axis)
+        array = jnp.sum(lax.all_gather(array, axis), axis=0)
     return array
 
 

time: 396 us -> 415 us (1.048)
  blocking collectives: 63.7 us -> 77.8 us
  starting transfers between devices: 22.8 us -> 27.8 us
    all_gather x0 -> x10, blocking collectives: none -> 77.8 us  [one_axis_at_a_time(): array = jnp.sum(lax.all_gather(array, axis), axis=0)]
    psum x5 -> x0, blocking collectives: 63.7 us -> none  [one_axis_at_a_time(): array = lax.psum(array, axis)]
    all_to_all x1, starting transfers between devices: 4.69 us -> 9.62 us  [move_rows(): lax.all_to_all(rows[ordering], HEAD_PTS, split_axis=0, concat_axis=0, til...]
  transfers between devices with their start and end apart: 3 -> 3, of which waited for: 1 -> 1; matrix products, arithmetic and copies ran while one was open for 61% -> 59% of each run, Pallas kernels for 0% -> 0%
where the time goes in v1:
time: 415 us; the launch traced here: 408 us
  local copies, waits for them, and re-layouts  133 us (32%)
  matrix products  105 us (25%)
  blocking collectives  77.8 us (19%)
  waiting for transfers between devices  33.3 us (8%)
  other arithmetic  29.5 us (7%)
  starting transfers between devices  27.8 us (7%)
    all_gather x10, blocking collectives, one_axis_at_a_time(): array = jnp.sum(lax.all_gather(array, axis), axis=0)  77.8 us
    dot_general x1, matrix products, finish_rows(): jnp.dot(normed_two, perceptron_entry_map, preferred_element_type=jnp.floa...  58.5 us
    gather x1, local copies, waits for them, and re-layouts, body(): inference_placement[ordering]  34.3 us
    gather x1, local copies, waits for them, and re-layouts, body(): anchor[ordering]  34.3 us
    all_to_all x1, waiting for transfers between devices, move_rows(): lax.all_to_all(rows[ordering], HEAD_PTS, split_axis=0, concat_axis=0, til...  33.3 us
    gather x1, local copies, waits for them, and re-layouts, move_rows(): return (arrived[placed], arrived_labels[placed, 1])  25.9 us
    gather x1, local copies, waits for them, and re-layouts, move_rows(): rows[ordering]  25.1 us
    dot_general x1, matrix products, finish_rows(): jnp.dot(inner_act, perceptron_exit_map, preferred_element_type=jnp.float32)  15.5 us
  transfers between devices with their start and end apart: 3, of which 1 were waited for; matrix products, arithmetic and copies ran while one was open for 59% of the time, Pallas kernels for 0%

profile of v1, /device:TPU:1, one launch (start us, length us, event | category | flops | bytes accessed | tf_op | source)
XLA Modules:
  0.0 407.6 jit_solution(14218376634625026899)
XLA Ops:
  1.3 6.9 %all-to-all-start = ((f32[8,1,2]{2,1,0:T(1,128)}), f32[8,1,2]{2,1,0:T(1,128)S(1)}, u32[]{:S(2)}, u32[]{:S(2)}) async-start(f32[8,1,2]{2,1,0:T(1,128)} %broadcast_in_dim.8), calls=%async_computation | async-start | bytes 8192 | tf_op jit(solution)/shard_map/all_to_all | solution.py:16
  8.2 4.6 %copy.45 = bf16[6144,256]{0,1:T(8,128)(2,1)} copy(bf16[6144,256]{1,0:T(8,128)(2,1)} %param.20) | data formatting | bytes 6291456 | tf_op args[0]
  12.8 2.6 convert_reduce_fusion
  15.4 2.7 fusion.27
  18.2 5.3 %convolution_convert_fusion.2 = bf16[6144,256]{0,1:T(8,128)(2,1)} fusion(bf16[256,256]{1,0:T(8,128)(2,1)S(1)} %copy-done.12, bf16[6144,256]{0,1:T(8,128)(2,1)} %copy.45, f32[256]{0:T(256)S(1)} %copy-done.19, f32[256]{0:T(256)S(1)} %copy-done.20, f32[6144]{0:T(1024)S(1)} %add_rsqrt_fusion.1, f32[6144]{0:T(1024)S(1)} %broadcast_multiply_fusion.1), kind=kOutput, calls=%fused_computation.36 | convolution fusion | flops 816316416 | bytes 6473728 | tf_op jit(solution)/shard_map/dot_general | solution.py:150
  23.5 3.4 convolution_convert_fusion.1
  27.0 6.7 %sort.34 = (s32[6144]{0:T(1024)}, s32[6144]{0:T(1024)S(1)}) sort(s32[6144]{0:T(1024)S(1)} %fusion.46, s32[6144]{0:T(1024)S(1)} %iota.11), dimensions={0}, to_apply=%region_19.20 | sort | flops 79872 | bytes 98304 | tf_op jit(solution)/shard_map/jit(argsort)/sort | solution.py:134
  33.7 34.3 %gather_fusion.1 = s32[6144]{0:T(1024)S(1)} fusion(s32[6144]{0:T(1024)S(1)} %copy-done.2, s32[6144]{0:T(1024)S(1)} %get-tuple-element.17), kind=kCustom, calls=%fused_computation.1 | custom fusion | bytes 73728 | tf_op jit(solution)/shard_map/gather | solution.py:136
  68.1 34.3 %gather_fusion.2 = s32[6144]{0:T(1024)S(1)} fusion(s32[6144]{0:T(1024)S(1)} %get-tuple-element.18, s32[6144]{0:T(1024)S(1)} %get-tuple-element.17), kind=kCustom, calls=%fused_computation.2 | custom fusion | bytes 73728 | tf_op jit(solution)/shard_map/gather | solution.py:136
  103.3 11.3 %all-to-all-start.2 = ((s32[128,48,2]{1,2,0:T(2,128)}), s32[128,48,2]{1,2,0:T(2,128)}, u32[]{:S(2)}, u32[]{:S(2)}) async-start(s32[128,48,2]{1,2,0:T(2,128)} %copy.52), calls=%async_computation.2 | async-start | bytes 262144 | tf_op jit(solution)/shard_map/all_to_all | solution.py:45
  115.9 10.9 %fusion.93 = (f32[6144,16]{0,1:T(8,128)S(1)}, f32[6144,16,32]{0,2,1:T(8,128)}) fusion(bf16[6144,16,16]{0,2,1:T(8,128)(2,1)} %bitcast.68, f32[16]{0:T(128)S(1)} %div.64, f32[32]{0:T(128)S(1)} %copy-done.24, bf16[16,32]{1,0:T(8,128)(2,1)S(1)} %copy-done.17), kind=kOutput, calls=%fused_computation.125 | convolution fusion | flops 113246240 | bytes 16123072 | tf_op jit(solution)/shard_map/sub | solution.py:160
  126.8 9.1 %fusion.31 = (f32[16,32]{1,0:T(8,128)S(1)}, bf16[6144,16,32]{0,2,1:T(8,128)(2,1)}) fusion(f32[6144,16,32]{0,2,1:T(8,128)} %get-tuple-element.12, f32[6144,16]{0,1:T(8,128)S(1)} %get-tuple-element.11), kind=kLoop, calls=%fused_computation.47 | loop fusion | flops 9436672 | bytes 19269632 | tf_op jit(solution)/shard_map/reduce_sum | solution.py:162
  135.8 4.6 %fusion.98 = f32[16,32,16]{1,2,0:T(8,128)S(1)} fusion(bf16[6144,16,32]{0,2,1:T(8,128)(2,1)} %get-tuple-element.10, bf16[6144,16,16]{0,2,1:T(8,128)(2,1)S(1)} %bitcast.56), kind=kOutput, calls=%fused_computation.128 | convolution fusion | flops 100663296 | bytes 9469952 | tf_op jit(solution)/shard_map/qct,qcv->ctv/dot_general | solution.py:163
  140.4 12.0 %all-gather = f32[64,32,16]{1,2,0:T(8,128)S(1)} all-gather(f32[16,32,16]{1,2,0:T(8,128)S(1)} %fusion.98), channel_id=2, replica_groups=mesh['head_0'=4,'head_1'=2,'pts_0'=2,'pts_1'=4,'pts_2'=2] {'head_0'}, dimensions={0}, use_global_device_ids=true | all-gather | bytes 163840 | tf_op jit(solution)/shard_map/all_gather | solution.py:32
  152.4 4.5 %all-gather.1 = f32[32,32,16]{1,2,0:T(8,128)S(1)} all-gather(f32[16,32,16]{1,2,0:T(8,128)S(1)} %reduce_sum.156), channel_id=3, replica_groups=mesh['head_0'=4,'head_1'=2,'pts_0'=2,'pts_1'=4,'pts_2'=2] {'head_1'}, dimensions={0}, use_global_device_ids=true | all-gather | bytes 98304 | tf_op jit(solution)/shard_map/all_gather | solution.py:32
  156.9 6.2 %all-gather.2 = f32[32,32,16]{1,2,0:T(8,128)S(1)} all-gather(f32[16,32,16]{1,2,0:T(8,128)S(1)} %reduce_sum.157), channel_id=4, replica_groups=mesh['head_0'=4,'head_1'=2,'pts_0'=2,'pts_1'=4,'pts_2'=2] {'pts_0'}, dimensions={0}, use_global_device_ids=true | all-gather | bytes 98304 | tf_op jit(solution)/shard_map/all_gather | solution.py:32
  163.2 10.6 %all-gather.3 = f32[64,32,16]{1,2,0:T(8,128)S(1)} all-gather(f32[16,32,16]{1,2,0:T(8,128)S(1)} %reduce_sum.158), channel_id=5, replica_groups=mesh['head_0'=4,'head_1'=2,'pts_0'=2,'pts_1'=4,'pts_2'=2] {'pts_1'}, dimensions={0}, use_global_device_ids=true | all-gather | bytes 163840 | tf_op jit(solution)/shard_map/all_gather | solution.py:32
  173.8 8.7 %all-gather.4 = f32[32,32,16]{1,2,0:T(8,128)S(1)} all-gather(f32[16,32,16]{1,2,0:T(8,128)S(1)} %reduce_sum.159), channel_id=6, replica_groups=mesh['head_0'=4,'head_1'=2,'pts_0'=2,'pts_1'=4,'pts_2'=2] {'pts_2'}, dimensions={0}, use_global_device_ids=true | all-gather | bytes 98304 | tf_op jit(solution)/shard_map/all_gather | solution.py:32
  182.5 9.4 %all-gather.5 = f32[64,32]{1,0:T(8,128)S(1)} all-gather(f32[16,32]{1,0:T(8,128)S(1)} %get-tuple-element.9), channel_id=7, replica_groups=mesh['head_0'=4,'head_1'=2,'pts_0'=2,'pts_1'=4,'pts_2'=2] {'head_0'}, dimensions={0}, use_global_device_ids=true | all-gather | bytes 10240 | tf_op jit(solution)/shard_map/all_gather | solution.py:32
  191.9 3.2 all-gather.6
  195.1 5.0 %all-gather.7 = f32[32,32]{1,0:T(8,128)S(1)} all-gather(f32[16,32]{1,0:T(8,128)S(1)} %reduce_sum.163), channel_id=9, replica_groups=mesh['head_0'=4,'head_1'=2,'pts_0'=2,'pts_1'=4,'pts_2'=2] {'pts_0'}, dimensions={0}, use_global_device_ids=true | all-gather | bytes 6144 | tf_op jit(solution)/shard_map/all_gather | solution.py:32
  200.1 9.2 %all-gather.8 = f32[64,32]{1,0:T(8,128)S(1)} all-gather(f32[16,32]{1,0:T(8,128)S(1)} %reduce_sum.164), channel_id=10, replica_groups=mesh['head_0'=4,'head_1'=2,'pts_0'=2,'pts_1'=4,'pts_2'=2] {'pts_1'}, dimensions={0}, use_global_device_ids=true | all-gather | bytes 10240 | tf_op jit(solution)/shard_map/all_gather | solution.py:32
  209.3 9.1 %all-gather.9 = f32[32,32]{1,0:T(8,128)S(1)} all-gather(f32[16,32]{1,0:T(8,128)S(1)} %reduce_sum.165), channel_id=11, replica_groups=mesh['head_0'=4,'head_1'=2,'pts_0'=2,'pts_1'=4,'pts_2'=2] {'pts_2'}, dimensions={0}, use_global_device_ids=true | all-gather | bytes 6144 | tf_op jit(solution)/shard_map/all_gather | solution.py:32
  220.5 3.8 convolution_convert_fusion
  228.4 58.5 %fusion.119 = bf16[6144,1024]{1,0:T(8,128)(2,1)} fusion(f32[1024]{0:T(1024)S(1)} %copy-done.18, bf16[256,1024]{1,0:T(8,128)(2,1)S(1)} %copy-done, f32[6144,256]{0,1:T(8,128)S(1)} %get-tuple-element.16, f32[256]{0:T(256)S(1)} %copy-done.21, f32[256]{0:T(256)S(1)} %copy-done.22, f32[6144]{0:T(1024)S(1)} %add_rsqrt_fusion, ...), kind=kOutput, calls=%fused_computation.8.clone.clone.clone.clone.clone.clone.clone.clone.1 | convolution fusion | flops 3644325888 | bytes 19453952 | tf_op jit(solution)/shard_map/dot_general | solution.py:95
  286.9 15.5 %fusion.22 = bf16[6144,256]{0,1:T(8,128)(2,1)} fusion(f32[6144,256]{0,1:T(8,128)} %copy-done.5, bf16[1024,256]{1,0:T(8,128)(2,1)S(1)} %copy-done.11, f32[256]{0:T(256)S(1)} %copy-done.23, bf16[6144,1024]{1,0:T(8,128)(2,1)} %fusion.119), kind=kOutput, calls=%fused_computation.37 | convolution fusion | flops 3225944064 | bytes 22545408 | tf_op jit(solution)/shard_map/dot_general | solution.py:101
  302.4 3.2 copy.51
  305.6 25.1 %gather_fusion = bf16[6144,256]{1,0:T(8,128)(2,1)} fusion(bf16[6144,256]{1,0:T(8,128)(2,1)S(1)} %copy.51, s32[6144]{0:T(1024)S(1)} %copy-done.8), kind=kCustom, calls=%fused_computation | custom fusion | bytes 6316032 | tf_op jit(solution)/shard_map/gather | solution.py:44
  330.7 9.6 %all-to-all-start.1 = ((bf16[128,48,256]{2,1,0:T(8,128)(2,1)}), bf16[128,48,256]{2,1,0:T(8,128)(2,1)}, u32[]{:S(2)}, u32[]{:S(2)}) async-start(bf16[128,48,256]{2,1,0:T(8,128)(2,1)} %bitcast.55), calls=%async_computation.1 | async-start | bytes 6291456 | tf_op jit(solution)/shard_map/all_to_all | solution.py:44
  341.4 6.7 %sort.35 = (s32[6144]{0:T(1024)}, s32[6144]{0:T(1024)S(1)}) sort(s32[6144]{0:T(1024)S(1)} %bitcast.64, s32[6144]{0:T(1024)S(1)} %iota.13), dimensions={0}, to_apply=%region_20.21 | sort | flops 79872 | bytes 98304 | tf_op jit(solution)/shard_map/jit(argsort)/sort | solution.py:46
  348.1 33.3 %all-to-all-done.1 = bf16[128,48,256]{2,1,0:T(8,128)(2,1)} async-done(((bf16[128,48,256]{2,1,0:T(8,128)(2,1)}), bf16[128,48,256]{2,1,0:T(8,128)(2,1)}, u32[]{:S(2)}, u32[]{:S(2)}) %all-to-all-start.1) | async-done | bytes 3145760 | tf_op jit(solution)/shard_map/all_to_all | solution.py:44
  381.4 25.9 %gather_fusion.3 = bf16[6144,256]{1,0:T(8,128)(2,1)} fusion(bf16[6144,256]{1,0:T(8,128)(2,1)} %bitcast.19, s32[6144]{0:T(1024)S(1)} %fusion.48), kind=kCustom, calls=%fused_computation.3 | custom fusion | bytes 6316032 | tf_op jit(solution)/shard_map/gather | solution.py:47
  (91 shorter events, 11.0 us)
Async XLA Ops:
  0.0 228.4 %copy-start = (bf16[256,1024]{1,0:T(8,128)(2,1)S(1)}, bf16[256,1024]{1,0:T(8,128)(2,1)}, u32[]{:S(2)}) copy-start(bf16[256,1024]{1,0:T(8,128)(2,1)} %param.36) | copy-start | bytes 1572868
  0.0 18.2 %copy-start.20 = (f32[256]{0:T(256)S(1)}, f32[256]{0:T(256)}, u32[]{:S(2)}) copy-start(f32[256]{0:T(256)} %param.22) | copy-start | bytes 3076
  0.0 18.2 %copy-start.19 = (f32[256]{0:T(256)S(1)}, f32[256]{0:T(256)}, u32[]{:S(2)}) copy-start(f32[256]{0:T(256)} %param.23) | copy-start | bytes 3076
  0.0 18.2 %copy-start.12 = (bf16[256,256]{1,0:T(8,128)(2,1)S(1)}, bf16[256,256]{1,0:T(8,128)(2,1)}, u32[]{:S(2)}) copy-start(bf16[256,256]{1,0:T(8,128)(2,1)} %param.25) | copy-start | bytes 393220
  1.3 102.0 %all-to-all-start = ((f32[8,1,2]{2,1,0:T(1,128)}), f32[8,1,2]{2,1,0:T(1,128)S(1)}, u32[]{:S(2)}, u32[]{:S(2)}) async-start(f32[8,1,2]{2,1,0:T(1,128)} %broadcast_in_dim.8), calls=%async_computation | async-start | bytes 8192 | tf_op jit(solution)/shard_map/all_to_all | solution.py:16
  12.8 10.7 %copy-start.3 = (bf16[6144,256]{0,1:T(8,128)(2,1)S(1)}, bf16[6144,256]{0,1:T(8,128)(2,1)}, u32[]{:S(2)}) copy-start(bf16[6144,256]{0,1:T(8,128)(2,1)} %copy.45) | copy-start | bytes 9437188
  12.8 10.7 %copy-start.13 = (bf16[256,256]{1,0:T(8,128)(2,1)S(1)}, bf16[256,256]{1,0:T(8,128)(2,1)}, u32[]{:S(2)}) copy-start(bf16[256,256]{1,0:T(8,128)(2,1)} %param.24) | copy-start | bytes 393220
  18.2 8.7 %copy-start.2 = (s32[6144]{0:T(1024)S(1)}, s32[6144]{0:T(1024)}, u32[]{:S(2)}) copy-start(s32[6144]{0:T(1024)} %param.21) | copy-start | bytes 73732
  33.7 34.3 %copy-start.7 = (s32[6144]{0:T(1024)}, s32[6144]{0:T(1024)S(1)}, u32[]{:S(2)}) copy-start(s32[6144]{0:T(1024)S(1)} %get-tuple-element.17) | copy-start | bytes 73732
  68.1 47.8 %copy-start.17 = (bf16[16,32]{1,0:T(8,128)(2,1)S(1)}, bf16[16,32]{1,0:T(8,128)(2,1)}, u32[]{:S(2)}) copy-start(bf16[16,32]{1,0:T(8,128)(2,1)} %param.26) | copy-start | bytes 3076
  68.1 47.8 %copy-start.24 = (f32[32]{0:T(128)S(1)}, f32[32]{0:T(128)}, u32[]{:S(2)}) copy-start(f32[32]{0:T(128)} %param.27) | copy-start | bytes 388
  103.3 227.4 %all-to-all-start.2 = ((s32[128,48,2]{1,2,0:T(2,128)}), s32[128,48,2]{1,2,0:T(2,128)}, u32[]{:S(2)}, u32[]{:S(2)}) async-start(s32[128,48,2]{1,2,0:T(2,128)} %copy.52), calls=%async_computation.2 | async-start | bytes 262144 | tf_op jit(solution)/shard_map/all_to_all | solution.py:45
  126.8 9.1 %copy-start.6 = (bf16[6144,256]{0,1:T(8,128)(2,1)S(1)}, bf16[6144,256]{0,1:T(8,128)(2,1)}, u32[]{:S(2)}) copy-start(bf16[6144,256]{0,1:T(8,128)(2,1)} %convolution_convert_fusion.1) | copy-start | bytes 9437188
  126.8 91.7 %copy-start.14 = (f32[16,16]{1,0:T(8,128)S(1)}, f32[16,16]{1,0:T(8,128)}, u32[]{:S(2)}) copy-start(f32[16,16]{1,0:T(8,128)} %param.30) | copy-start | bytes 3076
  126.8 92.0 %copy-start.15 = (f32[16,16]{1,0:T(8,128)S(1)}, f32[16,16]{1,0:T(8,128)}, u32[]{:S(2)}) copy-start(f32[16,16]{1,0:T(8,128)} %param.29) | copy-start | bytes 3076
  135.8 83.3 %copy-start.16 = (f32[16,16]{1,0:T(8,128)S(1)}, f32[16,16]{1,0:T(8,128)}, u32[]{:S(2)}) copy-start(f32[16,16]{1,0:T(8,128)} %param.31) | copy-start | bytes 3076
  135.8 88.5 %copy-start.9 = (bf16[256,256]{1,0:T(8,128)(2,1)S(1)}, bf16[256,256]{1,0:T(8,128)(2,1)}, u32[]{:S(2)}) copy-start(bf16[256,256]{1,0:T(8,128)(2,1)} %param.32) | copy-start | bytes 393220
  135.8 88.5 %copy-start.10 = (f32[256]{0:T(256)S(1)}, f32[256]{0:T(256)}, u32[]{:S(2)}) copy-start(f32[256]{0:T(256)} %param.33) | copy-start | bytes 3076
  218.4 5.9 %copy-start.4 = (bf16[6144,256]{0,1:T(8,128)(2,1)S(1)}, bf16[6144,256]{0,1:T(8,128)(2,1)}, u32[]{:S(2)}) copy-start(bf16[6144,256]{0,1:T(8,128)(2,1)} %copy.45) | copy-start | bytes 9437188
  224.3 4.1 %copy-start.18 = (f32[1024]{0:T(1024)S(1)}, f32[1024]{0:T(1024)}, u32[]{:S(2)}) copy-start(f32[1024]{0:T(1024)} %param.37) | copy-start | bytes 12292
  224.3 4.1 %copy-start.21 = (f32[256]{0:T(256)S(1)}, f32[256]{0:T(256)}, u32[]{:S(2)}) copy-start(f32[256]{0:T(256)} %param.35) | copy-start | bytes 3076
  224.3 4.1 %copy-start.22 = (f32[256]{0:T(256)S(1)}, f32[256]{0:T(256)}, u32[]{:S(2)}) copy-start(f32[256]{0:T(256)} %param.34) | copy-start | bytes 3076
  225.8 2.6 copy-start.5
  228.4 58.5 %copy-start.11 = (bf16[1024,256]{1,0:T(8,128)(2,1)S(1)}, bf16[1024,256]{1,0:T(8,128)(2,1)}, u32[]{:S(2)}) copy-start(bf16[1024,256]{1,0:T(8,128)(2,1)} %param.38) | copy-start | bytes 1572868
  228.4 58.5 %copy-start.23 = (f32[256]{0:T(256)S(1)}, f32[256]{0:T(256)}, u32[]{:S(2)}) copy-start(f32[256]{0:T(256)} %param.39) | copy-start | bytes 3076
  286.9 18.7 %copy-start.8 = (s32[6144]{0:T(1024)S(1)}, s32[6144]{0:T(1024)}, u32[]{:S(2)}) copy-start(s32[6144]{0:T(1024)} %copy-done.7) | copy-start | bytes 73732
  330.7 50.7 %all-to-all-start.1 = ((bf16[128,48,256]{2,1,0:T(8,128)(2,1)}), bf16[128,48,256]{2,1,0:T(8,128)(2,1)}, u32[]{:S(2)}, u32[]{:S(2)}) async-start(bf16[128,48,256]{2,1,0:T(8,128)(2,1)} %bitcast.55), calls=%async_computation.1 | async-start | bytes 6291456 | tf_op jit(solution)/shard_map/all_to_all | solution.py:44
  381.4 25.9 %copy-start.1 = (bf16[256,1024]{1,0:T(8,128)(2,1)S(1)}, bf16[256,1024]{1,0:T(8,128)(2,1)}, u32[]{:S(2)}) copy-start(bf16[256,1024]{1,0:T(8,128)(2,1)} %param.36) | copy-start | bytes 1572868
